TPU v7x, 128 devices: a whole 4x4x4 slice. The times are simulated.
128 devices in a mesh: section: 2 (over core), tp: 4 (over x), pool: 16 (over z, y).
Axes of the slice: x: 4, y: 4, z: 4, core: 2. Of those that a mesh axis runs over, the one named last changes fastest.
Arguments:
- hidden: bfloat16 [2, 16, 128, 8192], P('section', 'pool', None, 'tp'), may hold values from -6 to 6
- queries: bfloat16 [2, 16, 16, 8, 64, 128], P('section', 'pool', None, None, 'tp'), may hold values from -450 to 450, as said below
- window_key_value: bfloat16 [2, 16, 16, 2, 8, 8, 128], P('section', 'pool', None, None, 'tp'), may hold values from -12 to 12
- cached_key_value: bfloat16 [2, 16, 128, 2, 8, 64, 128], P('section', 'pool', None, None, 'tp'), may hold values from -12 to 12
- cached_length: int32 [2, 16, 16], P('section', 'pool'), may hold values from 1 to 1024, 6144 in all within a row
- request_page_table: int32 [2, 16, 16, 16], P('section', 'pool'), may hold values from 0 to 127
- request_adapter: int32 [2, 16, 16], replicated, may hold values from 0 to 127, as said below
- layer_page_slot: int32 [256], replicated, may hold values from 0 to 255, as said below
- wo: bfloat16 [2, 8192, 8192], P('section', 'tp'), may hold values from -0.09375 to 0.09375
- adapter_down: bfloat16 [256, 64, 8192], P(('section', 'pool'), None, 'tp'), may hold values from -0.0625 to 0.0625
- adapter_up: bfloat16 [256, 64, 8192], P(('section', 'pool'), None, 'tp'), may hold values from -0.75 to 0.75
Outputs:
- next_hidden: bfloat16 [2, 16, 128, 8192], P('section', 'pool', None, 'tp')
Inputs may be any that keep to these rules, and one draw needn't show every extreme that they name: `queries`: queries of order one; some entries far larger in the hidden draw. `request_page_table`: several requests may name the same cache page; entries past a request's length are read but excluded. `cached_length`: each request of a device has 1 to 1024 cached positions. `layer_page_slot`: the adapters of layer s occupy slots s * 128 to (s + 1) * 128 - 1, each slot once; slot q lies on the index q // 8 of section and pool taken together, section first, so layer s's pages sit on section s. `request_adapter`: up to all 16 requests of a pool group may use adapters held on one pool index, and one pool index may serve every request of its section.
All inputs are finite; a program needn't handle non-finite values.
Results may differ from a plain program's by a relative error of at most 0.009.
Values may be sent and summed in bfloat16 or wider, within the bound.
A program may use at most 192 MiB of HBM per device.

v0:
```python
import jax
import jax.numpy as jnp
from jax import lax
from jax.sharding import PartitionSpec as P


def from_behind(value, axis, steps):
    count = lax.axis_size(axis)
    pairs = [(source, (source + steps) % count) for source in range(count)]
    return lax.ppermute(value, axis, pairs)


def attend(queries, cache_pages, window_kv, lengths, page_rows):
    requests, window, head_count, head_size = queries.shape
    kv_heads = window_kv.shape[2]
    page_tok = cache_pages.shape[3]
    max_pages = page_rows.shape[1]
    cached = max_pages * page_tok
    picked = jnp.take(cache_pages, page_rows, axis=0)
    picked = jnp.transpose(picked, (0, 2, 3, 1, 4, 5)).reshape(
        requests, 2, kv_heads, cached, head_size
    )
    keys_all = jnp.concatenate([picked, window_kv], axis=3)
    grouped = queries.reshape(requests, window, kv_heads, head_count // kv_heads, head_size)
    scores = jnp.einsum(
        "rwkgd,rktd->rkgwt", grouped, keys_all[:, 0], preferred_element_type=jnp.float32
    ) * head_size ** (-0.5)
    position = jnp.arange(cached + window, dtype=jnp.int32)
    query_pos = jnp.arange(window, dtype=jnp.int32)
    in_cache = position[None, :] < lengths[:, None]
    in_window = (position[None, :] >= cached) & (position[None, :] - cached <= query_pos[:, None])
    allowed = in_cache[:, None, :] | in_window[None, :, :]
    scores = jnp.where(allowed[:, None, None, :, :], scores, -jnp.inf)
    largest = jnp.max(scores, axis=-1, keepdims=True)
    weights = jnp.exp(scores - largest)
    probs = (weights / jnp.sum(weights, axis=-1, keepdims=True)).astype(jnp.bfloat16)
    context = jnp.einsum(
        "rkgwt,rktd->rwkgd", probs, keys_all[:, 1], preferred_element_type=jnp.float32
    )
    return context.reshape(requests, window, head_count * head_size).astype(jnp.bfloat16)


def per_device(
    hidden,
    queries,
    window_key_value,
    cached_key_value,
    cached_length,
    request_page_table,
    request_adapter,
    layer_page_slot,
    wo,
    adapter_down,
    adapter_up,
):
    section_count = lax.axis_size("section")
    section_index = lax.axis_index("section")
    pool_index = lax.axis_index("pool")
    context = attend(
        queries[0, 0],
        cached_key_value[0, 0],
        window_key_value[0, 0],
        cached_length[0, 0],
        request_page_table[0, 0],
    )
    requests, window, width_of_head = context.shape
    flat_rows = context.reshape(requests * window, width_of_head)
    partial_out = jnp.dot(flat_rows, wo[0], preferred_element_type=jnp.float32)
    plain_output = lax.psum_scatter(partial_out, "tp", scatter_dimension=1, tiled=True)
    pages_per_member = adapter_down.shape[0]
    rank_width = adapter_down.shape[1]
    output_width = adapter_up.shape[2]
    adapters = layer_page_slot.shape[0] // section_count
    layer_start = section_index * adapters
    everyone = lax.all_gather(context, "pool", axis=0, tiled=True)
    total_requests = everyone.shape[0]
    all_slots = layer_page_slot[layer_start + request_adapter[section_index]].reshape(
        total_requests
    )
    local_slot = all_slots - layer_start - pool_index * pages_per_member
    owned_mask = (
        local_slot[:, None] == jnp.arange(pages_per_member, dtype=jnp.int32)[None, :]
    ).astype(jnp.float32)
    stacked_down = adapter_down.reshape(pages_per_member * rank_width, width_of_head)
    wide_rank = lax.dot_general(
        everyone, stacked_down, (((2,), (1,)), ((), ())), preferred_element_type=jnp.float32
    )
    wide_rank = wide_rank.reshape(total_requests, window, pages_per_member, rank_width)
    rank_hidden = jnp.sum(wide_rank * owned_mask[:, None, :, None], axis=2)
    rank_hidden = lax.psum(rank_hidden, "tp")
    broadcast_rows = (
        rank_hidden.astype(jnp.bfloat16)[:, :, None, :]
        * owned_mask.astype(jnp.bfloat16)[:, None, :, None]
    )
    broadcast_rows = broadcast_rows.reshape(total_requests * window, pages_per_member * rank_width)
    product = jnp.dot(
        broadcast_rows,
        adapter_up.reshape(pages_per_member * rank_width, output_width),
        preferred_element_type=jnp.float32,
    )
    returned = lax.all_to_all(
        product.astype(jnp.bfloat16), "pool", split_axis=0, concat_axis=0, tiled=True
    )
    adapter_delta = jnp.sum(
        returned.reshape(-1, requests * window, output_width).astype(jnp.float32), axis=0
    )
    blended_output = (hidden[0, 0].astype(jnp.float32) + plain_output + adapter_delta).astype(
        jnp.bfloat16
    )
    handed = from_behind(blended_output, "section", 1)
    return handed[None, None]


def solution(mesh):
    return jax.shard_map(
        per_device,
        mesh=mesh,
        in_specs=(
            P("section", "pool", None, "tp"),
            P("section", "pool", None, None, "tp", None),
            P("section", "pool", None, None, "tp", None, None),
            P("section", "pool", None, None, "tp", None, None),
            P("section", "pool", None),
            P("section", "pool", None, None),
            P(),
            P(),
            P("section", "tp", None),
            P(("section", "pool"), None, "tp"),
            P(("section", "pool"), None, "tp"),
        ),
        out_specs=P("section", "pool", None, "tp"),
        check_vma=False,
    )
```

profile of v0, /device:TPU:35, one launch (start us, length us, event | category | flops | bytes accessed | tf_op | source)
XLA Modules:
  0.0 320.7 jit_solution(6340486119828184799)
XLA Ops:
  7.4 0.8 compare_select_fusion.1
  8.2 0.7 compare_and_fusion
  8.9 0.1 reshape.214
  9.0 0.9 copy.45
  9.9 0.7 iota_compare_fusion
  10.7 13.1 %gather_fusion = bf16[256,2,2,64,128]{4,3,2,1,0:T(8,128)(2,1)} fusion(bf16[128,2,2,64,128]{4,3,2,1,0:T(8,128)(2,1)} %bitcast.82, s32[1024]{0:T(1024)S(1)} %pad_clamp_fusion.1), kind=kCustom, calls=%fused_computation | custom fusion | bytes 33555456 | tf_op jit(solution)/shard_map/jit(_take)/gather | solution.py:19
  23.8 14.2 %copy_select_fusion = bf16[16,16,2,2,64,128]{5,4,1,3,0,2:T(8,128)(2,1)} fusion(bf16[16,16,2,2,64,128]{5,4,3,2,1,0:T(8,128)(2,1)} %bitcast.81, pred[16,16]{1,0:T(8,128)(4,1)S(1)} %compare_and_fusion), kind=kLoop, calls=%fused_computation.7 | loop fusion | flops 8388608 | bytes 33554688 | tf_op jit(solution)/shard_map/jit(_take)/select_n | solution.py:19
  38.0 0.1 broadcast_or_fusion
  38.1 8.2 %fusion.36 = (f32[16,2,8,8]{2,3,1,0:T(8,128)S(1)}, f32[16,2,8,8,1032]{4,2,3,1,0:T(8,128)}) fusion(pred[16,8,1032]{2,1,0:T(8,128)(4,1)S(1)} %broadcast_or_fusion, bf16[16,2,2,8,128]{4,3,2,0,1:T(8,128)(2,1)S(1)} %bitcast.89, bf16[16,2,2,1024,128]{4,3,2,0,1:T(8,128)(2,1)} %bitcast.83, bf16[1,1,16,8,16,128]{5,4,3,2,1,0:T(8,128)(2,1)S(1)} %copy-done.3), kind=kOutput, calls=%fused_computation.56 | convolution fusion | flops 566428672 | bytes 26027008 | tf_op jit(solution)/shard_map/sub | solution.py:35
  46.3 7.1 %divide_convert_fusion = bf16[16,2,8,8,1032]{4,2,3,1,0:T(8,128)(2,1)} fusion(f32[16,2,8,8,1032]{4,2,3,1,0:T(8,128)} %get-tuple-element.8, f32[16,2,8,8]{2,3,1,0:T(8,128)S(1)} %get-tuple-element.7), kind=kLoop, calls=%fused_computation.10 | loop fusion | flops 4227072 | bytes 12689408 | tf_op jit(solution)/shard_map/convert_element_type | solution.py:36
  53.5 6.3 %fusion.21 = bf16[16,2,128,8,8]{2,4,3,1,0:T(8,128)(2,1)S(1)} fusion(bf16[16,2,8,8,1032]{4,2,3,1,0:T(8,128)(2,1)} %divide_convert_fusion, bf16[16,2,2,1024,128]{4,3,2,0,1:T(8,128)(2,1)} %bitcast.84, bf16[16,2,2,8,128]{4,3,2,0,1:T(8,128)(2,1)S(1)} %bitcast.90), kind=kOutput, calls=%fused_computation.30 | convolution fusion | flops 558235648 | bytes 21659648 | tf_op jit(solution)/shard_map/rkgwt,rktd->rwkgd/dot_general | solution.py:37
  59.7 1.1 copy.27
  60.9 0.1 reshape.222
  61.0 1.9 gather_fusion.1
  63.0 0.1 copy.29
  63.1 70.5 %all-gather.2.cloned.1.call-done = bf16[256,8,2048]{2,0,1:T(8,128)(2,1)} async-done(((bf16[16,8,2048]{2,0,1:T(8,128)(2,1)}), bf16[256,8,2048]{2,0,1:T(8,128)(2,1)}) %all-gather.2.cloned.1.call-update) | async-done | bytes 8388624 | tf_op jit(solution)/shard_map/all_gather | solution.py:75
  133.5 8.5 %multiply_reduce_fusion = f32[256,8,64]{0,2,1:T(8,128)S(1)} fusion(bf16[256,8,2048]{2,0,1:T(8,128)(2,1)} %all-gather.2.cloned.1.call-done, bf16[8,64,2048]{2,1,0:T(8,128)(2,1)} %param.20, f32[256,8]{0,1:T(8,128)S(1)} %get-tuple-element.5), kind=kOutput, calls=%fused_computation.27 | convolution fusion | flops 4296933376 | bytes 11018240 | tf_op jit(solution)/shard_map/dot_general | solution.py:85
  142.1 17.1 %all-reduce.1 = bf16[256,8,64]{0,2,1:T(8,128)(2,1)S(1)} all-reduce(f32[256,8,64]{0,2,1:T(8,128)S(1)} %multiply_reduce_fusion), channel_id=1, replica_groups=mesh['section'=2,'tp'=4,'pool'=16] {'tp'}, use_global_device_ids=true, to_apply=%region_4.5 | all-reduce | flops 131072 | bytes 786432 | tf_op jit(solution)/shard_map/psum | solution.py:90
  159.2 0.3 copy.28
  159.5 2.3 broadcast_multiply_fusion
  161.8 6.5 %mul.56 = bf16[2048,512]{1,0:T(8,128)(2,1)} reshape(bf16[256,8,8,64]{3,2,1,0:T(8,128)(2,1)} %broadcast_multiply_fusion) | data formatting | bytes 4194304 | tf_op jit(solution)/shard_map/mul | solution.py:92
  168.3 8.4 %convolution_convert_fusion = bf16[2048,2048]{1,0:T(8,128)(2,1)} fusion(bf16[2048,512]{1,0:T(8,128)(2,1)} %mul.56, bf16[512,2048]{1,0:T(8,128)(2,1)S(1)} %bitcast.80), kind=kOutput, calls=%fused_computation.22 | convolution fusion | flops 4299161600 | bytes 12582912 | tf_op jit(solution)/shard_map/dot_general | solution.py:96
  176.7 5.3 %all-to-all-start = ((bf16[16,128,2048]{2,1,0:T(8,128)(2,1)}), bf16[16,128,2048]{2,1,0:T(8,128)(2,1)}, u32[]{:S(2)}, u32[]{:S(2)}) async-start(bf16[16,128,2048]{2,1,0:T(8,128)(2,1)} %bitcast.85), calls=%async_computation.1 | async-start | bytes 16777216 | tf_op jit(solution)/shard_map/all_to_all | solution.py:101
  182.0 0.0 reduce-scatter.2.cloned.1.call-start
  182.0 17.0 %fusion.1 = f32[128,8192]{1,0:T(8,128)} fusion(bf16[128,2048]{1,0:T(8,128)(2,1)S(1)} %bitcast.87, bf16[1,2048,8192]{2,1,0:T(8,128)(2,1)} %param.19), kind=kOutput, calls=%fused_computation.3 | convolution fusion | flops 4294967296 | bytes 38273024 | tf_op jit(solution)/shard_map/dot_general | solution.py:68
  199.1 100.1 %all-to-all-done = bf16[16,128,2048]{2,1,0:T(8,128)(2,1)} async-done(((bf16[16,128,2048]{2,1,0:T(8,128)(2,1)}), bf16[16,128,2048]{2,1,0:T(8,128)(2,1)}, u32[]{:S(2)}, u32[]{:S(2)}) %all-to-all-start) | async-done | bytes 8388640 | tf_op jit(solution)/shard_map/all_to_all | solution.py:101
  299.2 5.3 %convert_reduce_fusion = f32[128,2048]{1,0:T(8,128)S(1)} fusion(bf16[16,128,2048]{2,1,0:T(8,128)(2,1)} %all-to-all-done), kind=kLoop, calls=%fused_computation.8 | loop fusion | flops 8126464 | bytes 9437184 | tf_op jit(solution)/shard_map/reduce_sum | solution.py:104
  304.5 0.0 reduce-scatter.2.cloned.1.call-done
  304.5 1.5 fusion.27
  306.1 4.9 %collective-permute-start = (bf16[128,2048]{1,0:T(8,128)(2,1)S(1)}, bf16[128,2048]{1,0:T(8,128)(2,1)S(1)}, u32[]{:S(2)}, u32[]{:S(2)}) collective-permute-start(bf16[128,2048]{1,0:T(8,128)(2,1)S(1)} %fusion.27), channel_id=1, source_target_pairs={{0,64},{64,0},{1,65},{65,1},{2,66},{66,2},{3,67},{67,3},{4,68},{68... | collective-permute-start | bytes 1572872 | tf_op jit(solution)/shard_map/ppermute | solution.py:10
  311.0 1.5 collective-permute-done
  312.5 0.8 copy.49
  (19 shorter events, 0.1 us)
Async XLA Ops:
  7.4 160.9 %copy-start = (bf16[8,64,2048]{2,1,0:T(8,128)(2,1)S(1)}, bf16[8,64,2048]{2,1,0:T(8,128)(2,1)}, u32[]{:S(2)}) copy-start(bf16[8,64,2048]{2,1,0:T(8,128)(2,1)} %param.21) | copy-start | bytes 6291460
  7.4 126.2 %all-gather.2.cloned.1.call-start = ((), (), s32[]{:S(2)}) async-start(), calls=%async_computation.3 | async-start | bytes 8912896 | tf_op jit(solution)/shard_map/all_gather | solution.py:75
  23.8 14.3 %copy-start.3 = (bf16[1,1,16,8,16,128]{5,4,3,2,1,0:T(8,128)(2,1)S(1)}, bf16[1,1,16,8,16,128]{5,4,3,2,1,0:T(8,128)(2,1)}, u32[]{:S(2)}) copy-start(bf16[1,1,16,8,16,128]{5,4,3,2,1,0:T(8,128)(2,1)} %param.12) | copy-start | bytes 1572868
  53.5 7.4 %copy-start.2 = (s32[2,16,16]{2,1,0:T(8,128)S(1)}, s32[2,16,16]{2,1,0:T(8,128)}, u32[]{:S(2)}) copy-start(s32[2,16,16]{2,1,0:T(8,128)} %param.17) | copy-start | bytes 6148
  53.5 7.5 %copy-start.1 = (s32[256]{0:T(256)S(1)}, s32[256]{0:T(256)}, u32[]{:S(2)}) copy-start(s32[256]{0:T(256)} %param.18) | copy-start | bytes 3076
  176.7 122.5 %all-to-all-start = ((bf16[16,128,2048]{2,1,0:T(8,128)(2,1)}), bf16[16,128,2048]{2,1,0:T(8,128)(2,1)}, u32[]{:S(2)}, u32[]{:S(2)}) async-start(bf16[16,128,2048]{2,1,0:T(8,128)(2,1)} %bitcast.85), calls=%async_computation.1 | async-start | bytes 16777216 | tf_op jit(solution)/shard_map/all_to_all | solution.py:101
  182.0 122.5 %reduce-scatter.2.cloned.1.call-start = ((), (), s32[]{:S(2)}) async-start(), calls=%async_computation.2 | async-start | bytes 5242880 | tf_op jit(solution)/shard_map/reduce_scatter | solution.py:69
  306.1 6.5 %collective-permute-start = (bf16[128,2048]{1,0:T(8,128)(2,1)S(1)}, bf16[128,2048]{1,0:T(8,128)(2,1)S(1)}, u32[]{:S(2)}, u32[]{:S(2)}) collective-permute-start(bf16[128,2048]{1,0:T(8,128)(2,1)S(1)} %fusion.27), channel_id=1, source_target_pairs={{0,64},{64,0},{1,65},{65,1},{2,66},{66,2},{3,67},{67,3},{4,68},{68... | collective-permute-start | bytes 1572872 | tf_op jit(solution)/shard_map/ppermute | solution.py:10
Sparse Core Ops, SparseCore 0:
  61.0 72.5 all-gather.1
Sparse Core Ops, SparseCore 1:
  199.1 51.5 reduce-scatter.1
where the time goes:
time: 321 us
  waiting for transfers between devices  172 us (54%)
  matrix products  48.3 us (15%)
  other arithmetic  32.9 us (10%)
  local copies, waits for them, and re-layouts  25 us (8%)
  blocking collectives  17.1 us (5%)
  between operations  15 us (5%)
  starting transfers between devices  10.3 us (3%)
    all_to_all x1, waiting for transfers between devices, per_device(): lax.all_to_all(product.astype(jnp.bfloat16), 'pool', split_axis=0, concat...  100 us
    all_gather x1, waiting for transfers between devices, per_device(): everyone = lax.all_gather(context, 'pool', axis=0, tiled=True)  70.5 us
    psum x1, blocking collectives, per_device(): rank_hidden = lax.psum(rank_hidden, 'tp')  17.1 us
    dot_general x1, matrix products, per_device(): partial_out = jnp.dot(flat_rows, wo[0], preferred_element_type=jnp.float32)  17 us
    select_n x2, other arithmetic, attend(): picked = jnp.take(cache_pages, page_rows, axis=0)  15 us
    gather x1, local copies, waits for them, and re-layouts, attend(): picked = jnp.take(cache_pages, page_rows, axis=0)  13.1 us
    dot_general x1, matrix products, per_device(): lax.dot_general(everyone, stacked_down, (((2,), (1,)), ((), ())), preferr...  8.55 us
    dot_general x1, matrix products, per_device(): jnp.dot(broadcast_rows, adapter_up.reshape(pages_per_member * rank_width,...  8.36 us
  transfers between devices with their start and end apart: 4, of which 3 were waited for; matrix products, arithmetic and copies ran while one was open for 8% of the time, Pallas kernels for 0%

commit v1 on v0

--- a/solution.py
+++ b/solution.py
@@ -72,7 +72,9 @@
     output_width = adapter_up.shape[2]
     adapters = layer_page_slot.shape[0] // section_count
     layer_start = section_index * adapters
-    everyone = lax.all_gather(context, "pool", axis=0, tiled=True)
+    everyone = jnp.concatenate(
+        lax.all_to_all(jnp.stack([context] * lax.axis_size("pool")), "pool", 0, 0), axis=0
+    )
     total_requests = everyone.shape[0]
     all_slots = layer_page_slot[layer_start + request_adapter[section_index]].reshape(
         total_requests

time: 321 us -> 391 us (1.22)
  waiting for transfers between devices: 172 us -> 222 us
  local copies, waits for them, and re-layouts: 25 us -> 36.9 us
  starting transfers between devices: 10.3 us -> 19.3 us
    all_to_all x0 -> x1, waiting for transfers between devices: none -> 120 us  [per_device(): lax.all_to_all(jnp.stack([context] * lax.axis_size('pool')), 'pool', 0, 0)]
    all_gather x1 -> x0, waiting for transfers between devices: 70.5 us -> none  [per_device(): everyone = lax.all_gather(context, 'pool', axis=0, tiled=True)]
    all_to_all x0 -> x1, local copies, waits for them, and re-layouts: none -> 8.4 us  [per_device(): lax.all_to_all(jnp.stack([context] * lax.axis_size('pool')), 'pool', 0, 0)]
    all_to_all x0 -> x1, starting transfers between devices: none -> 7.63 us  [per_device(): lax.all_to_all(jnp.stack([context] * lax.axis_size('pool')), 'pool', 0, 0)]
    another operation x0 -> x1, local copies, waits for them, and re-layouts: none -> 4.28 us  [per_device(): jnp.stack([context] * lax.axis_size('pool'))]
  transfers between devices with their start and end apart: 4 -> 4, of which waited for: 3 -> 3; matrix products, arithmetic and copies ran while one was open for 8% -> 6% of each run, Pallas kernels for 0% -> 0%
where the time goes in v1:
time: 391 us; the launch traced here: 390 us
  waiting for transfers between devices  222 us (57%)
  matrix products  48 us (12%)
  local copies, waits for them, and re-layouts  36.9 us (9%)
  other arithmetic  32.9 us (8%)
  starting transfers between devices  19.3 us (5%)
  blocking collectives  17.6 us (5%)
  between operations  13.5 us (3%)
    all_to_all x1, waiting for transfers between devices, per_device(): lax.all_to_all(jnp.stack([context] * lax.axis_size('pool')), 'pool', 0, 0)  120 us
    all_to_all x1, waiting for transfers between devices, per_device(): lax.all_to_all(product.astype(jnp.bfloat16), 'pool', split_axis=0, concat...  99.5 us
    psum x1, blocking collectives, per_device(): rank_hidden = lax.psum(rank_hidden, 'tp')  17.6 us
    dot_general x1, matrix products, per_device(): partial_out = jnp.dot(flat_rows, wo[0], preferred_element_type=jnp.float32)  17 us
    select_n x2, other arithmetic, attend(): picked = jnp.take(cache_pages, page_rows, axis=0)  15 us
    gather x1, local copies, waits for them, and re-layouts, attend(): picked = jnp.take(cache_pages, page_rows, axis=0)  13.1 us
    all_to_all x1, local copies, waits for them, and re-layouts, per_device(): lax.all_to_all(jnp.stack([context] * lax.axis_size('pool')), 'pool', 0, 0)  8.4 us
    dot_general x1, matrix products, per_device(): jnp.dot(broadcast_rows, adapter_up.reshape(pages_per_member * rank_width,...  8.36 us
  transfers between devices with their start and end apart: 4, of which 3 were waited for; matrix products, arithmetic and copies ran while one was open for 6% of the time, Pallas kernels for 0%

profile of v1, /device:TPU:35, one launch (start us, length us, event | category | flops | bytes accessed | tf_op | source)
XLA Modules:
  0.0 389.7 jit_solution(10763987690690736051)
XLA Ops:
  6.5 0.8 compare_select_fusion.1
  7.4 0.7 compare_and_fusion
  8.2 0.9 copy.46
  9.1 0.7 iota_compare_fusion
  9.8 13.1 %gather_fusion = bf16[256,2,2,64,128]{4,3,2,1,0:T(8,128)(2,1)} fusion(bf16[128,2,2,64,128]{4,3,2,1,0:T(8,128)(2,1)} %bitcast.81, s32[1024]{0:T(1024)S(1)} %pad_clamp_fusion.1), kind=kCustom, calls=%fused_computation | custom fusion | bytes 33555456 | tf_op jit(solution)/shard_map/jit(_take)/gather | solution.py:19
  23.0 14.2 %copy_select_fusion = bf16[16,16,2,2,64,128]{5,4,1,3,0,2:T(8,128)(2,1)} fusion(bf16[16,16,2,2,64,128]{5,4,3,2,1,0:T(8,128)(2,1)} %bitcast.80, pred[16,16]{1,0:T(8,128)(4,1)S(1)} %compare_and_fusion), kind=kLoop, calls=%fused_computation.7 | loop fusion | flops 8388608 | bytes 33554688 | tf_op jit(solution)/shard_map/jit(_take)/select_n | solution.py:19
  37.2 0.1 broadcast_or_fusion
  37.3 8.2 %fusion.32 = (f32[16,2,8,8]{2,3,1,0:T(8,128)S(1)}, f32[16,2,8,8,1032]{4,2,3,1,0:T(8,128)}) fusion(pred[16,8,1032]{2,1,0:T(8,128)(4,1)S(1)} %broadcast_or_fusion, bf16[16,2,2,8,128]{4,3,2,0,1:T(8,128)(2,1)S(1)} %bitcast.89, bf16[16,2,2,1024,128]{4,3,2,0,1:T(8,128)(2,1)} %bitcast.82, bf16[1,1,16,8,16,128]{5,4,3,2,1,0:T(8,128)(2,1)S(1)} %copy-done.4), kind=kOutput, calls=%fused_computation.54 | convolution fusion | flops 566428672 | bytes 26027008 | tf_op jit(solution)/shard_map/sub | solution.py:35
  45.5 7.1 %divide_convert_fusion = bf16[16,2,8,8,1032]{4,2,3,1,0:T(8,128)(2,1)} fusion(f32[16,2,8,8,1032]{4,2,3,1,0:T(8,128)} %get-tuple-element.8, f32[16,2,8,8]{2,3,1,0:T(8,128)S(1)} %get-tuple-element.7), kind=kLoop, calls=%fused_computation.10 | loop fusion | flops 4227072 | bytes 12689408 | tf_op jit(solution)/shard_map/convert_element_type | solution.py:36
  52.6 6.2 %fusion.17 = bf16[16,2,128,8,8]{2,4,3,1,0:T(8,128)(2,1)S(1)} fusion(bf16[16,2,8,8,1032]{4,2,3,1,0:T(8,128)(2,1)} %divide_convert_fusion, bf16[16,2,2,1024,128]{4,3,2,0,1:T(8,128)(2,1)} %bitcast.83, bf16[16,2,2,8,128]{4,3,2,0,1:T(8,128)(2,1)S(1)} %bitcast.90), kind=kOutput, calls=%fused_computation.28 | convolution fusion | flops 558235648 | bytes 21659648 | tf_op jit(solution)/shard_map/rkgwt,rktd->rwkgd/dot_general | solution.py:37
  58.9 0.3 copy.27
  59.2 4.3 %stack.2 = bf16[16,16,8,2048]{3,1,2,0:T(8,128)(2,1)} broadcast(bf16[16,8,2048]{2,0,1:T(8,128)(2,1)S(1)} %copy.27), dimensions={1,2,3} | broadcast | bytes 8912896 | tf_op jit(solution)/shard_map/stack | solution.py:76
  63.4 7.6 %all-to-all-start = ((bf16[16,16,8,2048]{3,1,2,0:T(8,128)(2,1)}), bf16[16,16,8,2048]{3,1,2,0:T(8,128)(2,1)}, u32[]{:S(2)}, u32[]{:S(2)}) async-start(bf16[16,16,8,2048]{3,1,2,0:T(8,128)(2,1)} %stack.2), calls=%async_computation.1 | async-start | bytes 16777216 | tf_op jit(solution)/shard_map/all_to_all | solution.py:76
  71.1 0.1 reshape.229
  71.2 1.9 gather_fusion.1
  73.2 0.1 copy.30
  73.3 120.4 %all-to-all-done = bf16[16,16,8,2048]{3,1,2,0:T(8,128)(2,1)} async-done(((bf16[16,16,8,2048]{3,1,2,0:T(8,128)(2,1)}), bf16[16,16,8,2048]{3,1,2,0:T(8,128)(2,1)}, u32[]{:S(2)}, u32[]{:S(2)}) %all-to-all-start) | async-done | bytes 8388640 | tf_op jit(solution)/shard_map/all_to_all | solution.py:76
  193.7 8.4 %copy.28 = bf16[16,16,8,2048]{3,1,0,2:T(8,128)(2,1)} copy(bf16[16,16,8,2048]{3,1,2,0:T(8,128)(2,1)} %all-to-all-done) | data formatting | bytes 16777216 | tf_op jit(solution)/shard_map/all_to_all | solution.py:76
  202.1 8.2 %multiply_reduce_fusion = f32[256,8,64]{0,2,1:T(8,128)S(1)} fusion(bf16[256,8,2048,1]{2,0,3,1:T(8,128)(2,1)} %bitcast.85, bf16[8,64,2048]{2,1,0:T(8,128)(2,1)S(1)} %copy-done.3, f32[256,8]{0,1:T(8,128)S(1)} %get-tuple-element.5), kind=kOutput, calls=%fused_computation.25 | convolution fusion | flops 4296933376 | bytes 11018240 | tf_op jit(solution)/shard_map/dot_general | solution.py:87
  210.3 17.6 %all-reduce.1 = bf16[256,8,64]{0,2,1:T(8,128)(2,1)S(1)} all-reduce(f32[256,8,64]{0,2,1:T(8,128)S(1)} %multiply_reduce_fusion), channel_id=1, replica_groups=mesh['section'=2,'tp'=4,'pool'=16] {'tp'}, use_global_device_ids=true, to_apply=%region_4.5 | all-reduce | flops 131072 | bytes 786432 | tf_op jit(solution)/shard_map/psum | solution.py:92
  227.9 0.3 copy.29
  228.2 2.3 broadcast_multiply_fusion
  230.5 6.5 %mul.56 = bf16[2048,512]{1,0:T(8,128)(2,1)} reshape(bf16[256,8,8,64]{3,2,1,0:T(8,128)(2,1)} %broadcast_multiply_fusion) | data formatting | bytes 4194304 | tf_op jit(solution)/shard_map/mul | solution.py:94
  237.0 8.4 %convolution_convert_fusion = bf16[2048,2048]{1,0:T(8,128)(2,1)} fusion(bf16[2048,512]{1,0:T(8,128)(2,1)} %mul.56, bf16[512,2048]{1,0:T(8,128)(2,1)S(1)} %bitcast.79), kind=kOutput, calls=%fused_computation.20 | convolution fusion | flops 4299161600 | bytes 12582912 | tf_op jit(solution)/shard_map/dot_general | solution.py:98
  245.4 6.1 %all-to-all-start.1 = ((bf16[16,128,2048]{2,1,0:T(8,128)(2,1)}), bf16[16,128,2048]{2,1,0:T(8,128)(2,1)}, u32[]{:S(2)}, u32[]{:S(2)}) async-start(bf16[16,128,2048]{2,1,0:T(8,128)(2,1)} %bitcast.84), calls=%async_computation.2 | async-start | bytes 16777216 | tf_op jit(solution)/shard_map/all_to_all | solution.py:103
  251.5 17.0 %fusion.1 = f32[128,8192]{1,0:T(8,128)} fusion(bf16[128,2048]{1,0:T(8,128)(2,1)S(1)} %bitcast.87, bf16[1,2048,8192]{2,1,0:T(8,128)(2,1)} %param.19), kind=kOutput, calls=%fused_computation.3 | convolution fusion | flops 4294967296 | bytes 38273024 | tf_op jit(solution)/shard_map/dot_general | solution.py:68
  268.5 99.5 %all-to-all-done.1 = bf16[16,128,2048]{2,1,0:T(8,128)(2,1)} async-done(((bf16[16,128,2048]{2,1,0:T(8,128)(2,1)}), bf16[16,128,2048]{2,1,0:T(8,128)(2,1)}, u32[]{:S(2)}, u32[]{:S(2)}) %all-to-all-start.1) | async-done | bytes 8388640 | tf_op jit(solution)/shard_map/all_to_all | solution.py:103
  368.1 5.3 %convert_reduce_fusion = f32[128,2048]{1,0:T(8,128)S(1)} fusion(bf16[16,128,2048]{2,1,0:T(8,128)(2,1)} %all-to-all-done.1), kind=kLoop, calls=%fused_computation.8 | loop fusion | flops 8126464 | bytes 9437184 | tf_op jit(solution)/shard_map/reduce_sum | solution.py:106
  373.4 1.5 fusion.23
  374.9 5.6 %collective-permute-start = (bf16[128,2048]{1,0:T(8,128)(2,1)S(1)}, bf16[128,2048]{1,0:T(8,128)(2,1)S(1)}, u32[]{:S(2)}, u32[]{:S(2)}) collective-permute-start(bf16[128,2048]{1,0:T(8,128)(2,1)S(1)} %fusion.23), channel_id=1, source_target_pairs={{0,64},{64,0},{1,65},{65,1},{2,66},{66,2},{3,67},{67,3},{4,68},{68... | collective-permute-start | bytes 1572872 | tf_op jit(solution)/shard_map/ppermute | solution.py:10
  380.5 1.5 collective-permute-done
  382.1 0.8 copy.50
  (22 shorter events, 0.2 us)
Async XLA Ops:
  6.5 230.5 %copy-start = (bf16[8,64,2048]{2,1,0:T(8,128)(2,1)S(1)}, bf16[8,64,2048]{2,1,0:T(8,128)(2,1)}, u32[]{:S(2)}) copy-start(bf16[8,64,2048]{2,1,0:T(8,128)(2,1)} %param.21) | copy-start | bytes 6291460
  23.0 14.3 %copy-start.4 = (bf16[1,1,16,8,16,128]{5,4,3,2,1,0:T(8,128)(2,1)S(1)}, bf16[1,1,16,8,16,128]{5,4,3,2,1,0:T(8,128)(2,1)}, u32[]{:S(2)}) copy-start(bf16[1,1,16,8,16,128]{5,4,3,2,1,0:T(8,128)(2,1)} %param.12) | copy-start | bytes 1572868
  63.4 7.6 %copy-start.2 = (s32[2,16,16]{2,1,0:T(8,128)S(1)}, s32[2,16,16]{2,1,0:T(8,128)}, u32[]{:S(2)}) copy-start(s32[2,16,16]{2,1,0:T(8,128)} %param.17) | copy-start | bytes 6148
  63.4 7.8 %copy-start.1 = (s32[256]{0:T(256)S(1)}, s32[256]{0:T(256)}, u32[]{:S(2)}) copy-start(s32[256]{0:T(256)} %param.18) | copy-start | bytes 3076
  63.4 130.3 %all-to-all-start = ((bf16[16,16,8,2048]{3,1,2,0:T(8,128)(2,1)}), bf16[16,16,8,2048]{3,1,2,0:T(8,128)(2,1)}, u32[]{:S(2)}, u32[]{:S(2)}) async-start(bf16[16,16,8,2048]{3,1,2,0:T(8,128)(2,1)} %stack.2), calls=%async_computation.1 | async-start | bytes 16777216 | tf_op jit(solution)/shard_map/all_to_all | solution.py:76
  193.7 8.4 %copy-start.3 = (bf16[8,64,2048]{2,1,0:T(8,128)(2,1)S(1)}, bf16[8,64,2048]{2,1,0:T(8,128)(2,1)}, u32[]{:S(2)}) copy-start(bf16[8,64,2048]{2,1,0:T(8,128)(2,1)} %param.20) | copy-start | bytes 6291460
  245.4 122.7 %all-to-all-start.1 = ((bf16[16,128,2048]{2,1,0:T(8,128)(2,1)}), bf16[16,128,2048]{2,1,0:T(8,128)(2,1)}, u32[]{:S(2)}, u32[]{:S(2)}) async-start(bf16[16,128,2048]{2,1,0:T(8,128)(2,1)} %bitcast.84), calls=%async_computation.2 | async-start | bytes 16777216 | tf_op jit(solution)/shard_map/all_to_all | solution.py:103
  251.4 121.9 %reduce-scatter.2.cloned.1.call-start = ((), (), s32[]{:S(2)}) async-start(), calls=%async_computation.3 | async-start | bytes 5242880 | tf_op jit(solution)/shard_map/reduce_scatter | solution.py:69
  374.9 7.1 %collective-permute-start = (bf16[128,2048]{1,0:T(8,128)(2,1)S(1)}, bf16[128,2048]{1,0:T(8,128)(2,1)S(1)}, u32[]{:S(2)}, u32[]{:S(2)}) collective-permute-start(bf16[128,2048]{1,0:T(8,128)(2,1)S(1)} %fusion.23), channel_id=1, source_target_pairs={{0,64},{64,0},{1,65},{65,1},{2,66},{66,2},{3,67},{67,3},{4,68},{68... | collective-permute-start | bytes 1572872 | tf_op jit(solution)/shard_map/ppermute | solution.py:10
Sparse Core Ops, SparseCore 0:
  268.6 51.9 reduce-scatter.1
